TPU v7x, 32 devices: a whole 2x2x4 slice. The times are simulated.
32 devices in a mesh: lat: 4 (over y, x), lon: 4 (over z), lev: 2 (over core).
Axes of the slice: x: 2, y: 2, z: 4, core: 2. Of those that a mesh axis runs over, the one named last changes fastest.
Arguments:
- field_values: float32 [16, 256, 192, 128], P('lat', 'lon', 'lev'), may hold values from 0.2 to 1.8
- crowding: float32 [16, 256, 192, 128], P('lat', 'lon', 'lev'), may hold values from 0.5 to 2
Outputs:
- field_values_end: float32 [16, 256, 192, 128], P('lat', 'lon', 'lev')
All inputs are finite; a program needn't handle non-finite values.
Results may differ from a plain program's by a relative error of at most 0.00002.
Values sent between devices are 32-bit elements; how exact they have to be, the bound alone decides.
A program may use at most 384 MiB of HBM per device.

v0:
```python
import functools
import math

import jax
import jax.numpy as jnp
from jax import lax
from jax.experimental import pallas as pl
from jax.experimental.pallas import tpu as pltpu
from jax.sharding import PartitionSpec as P

STEPS = 3
CHUNK_ROWS = 8
WINDOW = 3
MESH = pl.DeviceIdType.MESH
AXES = ("lat", "lon", "lev")


def march_kernel(sizes, shape, rows, f_in, c_in, odd, even, crowd, jh, kh, kf,
                 load_sems, j_send, j_recv, i_send, i_recv, k_send, k_recv):
    J, I, K, L = shape
    chunks = I // rows
    near = {}
    for axis, count in zip(AXES, sizes):
        me = lax.axis_index(axis)
        near[axis] = (lax.rem(me + count - 1, count), lax.rem(me + 1, count))

    barrier = pltpu.get_barrier_semaphore()
    for axis in AXES:
        for target in near[axis]:
            pl.semaphore_signal(barrier, inc=1, device_id={axis: target}, device_id_type=MESH)
    pl.semaphore_wait(barrier, 2 * len(AXES))

    fields = (even, odd)

    def remote(source, target, send, recv, axis, side):
        return pltpu.make_async_remote_copy(
            src_ref=source, dst_ref=target, send_sem=send, recv_sem=recv,
            device_id={axis: near[axis][side]}, device_id_type=MESH)

    def j_copy(step, side, chunk):
        j = (J - 1) * side
        if step == 0:
            source = f_in.at[j, pl.ds(chunk * rows, rows)]
        else:
            source = fields[step % 2].at[j, pl.ds(1 + chunk * rows, rows)]
        return remote(source, jh.at[step, 1 - side, pl.ds(chunk * rows, rows)],
                      j_send.at[step, side, chunk], j_recv.at[step, 1 - side, chunk], "lat", side)

    def i_copy(step, side):
        if step == 0:
            source = f_in.at[:, (I - 1) * side]
        else:
            source = fields[step % 2].at[:, 1 + (I - 1) * side]
        return remote(source, fields[step % 2].at[:, (I + 1) * (1 - side)],
                      i_send.at[step, side], i_recv.at[step, 1 - side], "lon", side)

    def k_copy(step, side):
        return remote(kf.at[step, side], kh.at[step, 1 - side],
                      k_send.at[step, side], k_recv.at[step, 1 - side], "lev", side)

    window = min(WINDOW, chunks - 1)

    @pl.loop(0, window)
    def _(chunk):
        for side in (0, 1):
            j_copy(0, side, chunk).start()

    for side in (0, 1):
        i_copy(0, side).start()
    load_f = pltpu.make_async_copy(f_in, even.at[:, pl.ds(1, I)], load_sems.at[0])
    load_c = pltpu.make_async_copy(c_in, crowd, load_sems.at[1])
    load_f.start()
    load_c.start()
    load_f.wait()

    @pl.loop(0, I)
    def _(i):
        for j in range(J):
            kf[0, 0, j, pl.ds(i, 1), :] = even[j, i + 1, 0:1, :]
            kf[0, 1, j, pl.ds(i, 1), :] = even[j, i + 1, K - 1:K, :]

    load_c.wait()
    for side in (0, 1):
        k_copy(0, side).start()

    at_k = lax.broadcasted_iota(jnp.int32, (K, L), 0)

    for step in range(STEPS):
        source, target = fields[step % 2], fields[(step + 1) % 2]
        last = step == STEPS - 1
        for side in (0, 1):
            i_copy(step, side).wait_recv()
            k_copy(step, side).wait_recv()
            if step >= 1:
                i_copy(step - 1, side).wait_send()

        @pl.loop(0, chunks)
        def _(chunk):
            for side in (0, 1):
                j_copy(step, side, chunk).wait_recv()
                j_copy(step, side, chunk).wait_send()

            @pl.when(chunk + window < chunks)
            def _():
                for side in (0, 1):
                    j_copy(step, side, chunk + window).start()

            if not last:
                @pl.when(chunk + window >= chunks)
                def _():
                    for side in (0, 1):
                        j_copy(step + 1, side, chunk + window - chunks).start()

            @pl.loop(0, rows)
            def _(row):
                i = chunk * rows + row
                for j in range(J):
                    middle = source[j, i + 1]
                    below = jh[step, 0, i] if j == 0 else source[j - 1, i + 1]
                    above = jh[step, 1, i] if j == J - 1 else source[j + 1, i + 1]
                    total = below + above + source[j, i] + source[j, i + 2]
                    total += jnp.where(at_k == 0, kh[step, 0, j, pl.ds(i, 1), :],
                                       pltpu.roll(middle, 1, 0))
                    total += jnp.where(at_k == K - 1, kh[step, 1, j, pl.ds(i, 1), :],
                                       pltpu.roll(middle, K - 1, 0))
                    new = middle * (0.6 - 0.2 * (middle * crowd[j, i])) + 0.1 * total
                    target[j, i + 1] = new
                    if not last:
                        kf[step + 1, 0, j, pl.ds(i, 1), :] = new[0:1]
                        kf[step + 1, 1, j, pl.ds(i, 1), :] = new[K - 1:K]

        if not last:
            for side in (0, 1):
                i_copy(step + 1, side).start()
                k_copy(step + 1, side).start()

    for side in (0, 1):
        i_copy(STEPS - 1, side).wait_send()
        for step in range(STEPS):
            k_copy(step, side).wait_send()


def write_kernel(shape, held, out, sems):
    J, I = shape[:2]
    copies = [pltpu.make_async_copy(held.at[j, pl.ds(1, I)], out.at[j], sems.at[j])
              for j in range(J)]
    for copy in copies:
        copy.start()
    for copy in copies:
        copy.wait()


def local(sizes, field_values, crowding):
    J, I, K, L = shape = field_values.shape
    rows = math.gcd(I, CHUNK_ROWS)
    chunks = I // rows
    dtype = field_values.dtype
    DMA = pltpu.SemaphoreType.DMA
    marched = pl.pallas_call(
        functools.partial(march_kernel, sizes, shape, rows),
        out_shape=pltpu.VMEM((J, I + 2, K, L), dtype),
        in_specs=[pl.BlockSpec(memory_space=pl.ANY)] * 2,
        out_specs=pl.BlockSpec(memory_space=pltpu.VMEM),
        scratch_shapes=[
            pltpu.VMEM((J, I + 2, K, L), dtype),
            pltpu.VMEM(shape, dtype),
            pltpu.VMEM((STEPS, 2, I, K, L), dtype),
            pltpu.VMEM((STEPS, 2, J, I, L), dtype),
            pltpu.VMEM((STEPS, 2, J, I, L), dtype),
            DMA((2,)),
            DMA((STEPS, 2, chunks)),
            DMA((STEPS, 2, chunks)),
            DMA((STEPS, 2)),
            DMA((STEPS, 2)),
            DMA((STEPS, 2)),
            DMA((STEPS, 2)),
        ],
        compiler_params=pltpu.CompilerParams(
            collective_id=0, has_side_effects=True, vmem_limit_bytes=50 * 1024 * 1024),
    )(field_values, crowding)
    return pl.pallas_call(
        functools.partial(write_kernel, shape),
        out_shape=jax.ShapeDtypeStruct(shape, dtype),
        in_specs=[pl.BlockSpec(memory_space=pltpu.VMEM)],
        out_specs=pl.BlockSpec(memory_space=pl.ANY),
        scratch_shapes=[DMA((J,))],
        compiler_params=pltpu.CompilerParams(vmem_limit_bytes=1024 * 1024),
    )(pltpu.with_memory_space_constraint(marched, pltpu.VMEM))


def solution(mesh):
    spec = P("lat", "lon", "lev", None)
    sizes = tuple(mesh.shape[axis] for axis in AXES)
    return jax.shard_map(
        functools.partial(local, sizes), mesh=mesh, in_specs=(spec, spec), out_specs=spec,
        check_vma=False,
    )
```

profile of v0, /device:TPU:1, one launch (start us, length us, event | category | flops | bytes accessed | tf_op | source)
XLA Modules:
  0.0 417.8 jit_solution(3191463610524947937)
XLA Ops:
  0.0 413.0 %shard_map.28.held = f32[4,66,96,128]{3,2,1,0:T(8,128)S(1)} custom-call(f32[4,64,96,128]{3,2,1,0:T(8,128)} %f_in.1, f32[4,64,96,128]{3,2,1,0:T(8,128)} %c_in.1), custom_call_target="tpu_custom_call" | custom-call | tf_op jit(solution)/shard_map/pallas_call | solution.py:159
  413.0 4.7 %shard_map.29 = f32[4,64,96,128]{3,2,1,0:T(8,128)} custom-call(f32[4,66,96,128]{3,2,1,0:T(8,128)S(1)} %shard_map.28.held), custom_call_target="tpu_custom_call" | custom-call | tf_op jit(solution)/shard_map/pallas_call | solution.py:181
where the time goes:
time: 419 us; the launch traced here: 418 us
  Pallas kernels  418 us (100%)
    pallas_call x1, Pallas kernels, local(): pl.pallas_call(functools.partial(march_kernel, sizes, shape, rows), out_s...  413 us

commit v1 on v0

v1 whole, which is shorter than its diff:
```python
import functools
import math

import jax
import jax.numpy as jnp
from jax import lax
from jax.experimental import pallas as pl
from jax.experimental.pallas import tpu as pltpu
from jax.sharding import PartitionSpec as P

STEPS = 3
CHUNK_ROWS = 8
WINDOW = 5
TAIL_CHUNKS = 2
PIECE_ROWS = 4
MESH = pl.DeviceIdType.MESH
AXES = ("lat", "lon", "lev")


def neighbours(sizes, axis):
    count, me = sizes[AXES.index(axis)], lax.axis_index(axis)
    return lax.rem(me + count - 1, count), lax.rem(me + 1, count)


def is_late(sizes):
    return lax.axis_index("lev") == sizes[AXES.index("lev")] - 1


def signal(sizes, axis, semaphore):
    for target in neighbours(sizes, axis):
        pl.semaphore_signal(semaphore, inc=1, device_id={axis: target}, device_id_type=MESH)


def enter(sizes, ready):
    barrier = pltpu.get_barrier_semaphore()
    second = {axis: lax.rem(lax.axis_index(axis), 2) == parity
              for axis, parity in (("lon", 1), ("lev", 0))}
    signal(sizes, "lat", barrier)
    pl.semaphore_wait(barrier, 2 + sum(2 * second[axis].astype(jnp.int32) for axis in second))

    def answer():
        for axis in second:
            pl.when(jnp.logical_not(second[axis]))(lambda: signal(sizes, axis, barrier))
            pl.when(second[axis])(lambda: signal(sizes, axis, ready.at[AXES.index(axis)]))

    def await_answer(axis):
        pl.when(jnp.logical_not(second[axis]))(
            lambda: pl.semaphore_wait(ready.at[AXES.index(axis)], 2))

    return answer, await_answer


def enter_together(sizes, axes):
    barrier = pltpu.get_barrier_semaphore()
    for axis in axes:
        signal(sizes, axis, barrier)
    pl.semaphore_wait(barrier, 2 * len(axes))


def march_kernel(sizes, shape, rows, tail, f_in, c_in, odd, even, crowd, jh, kh, kf,
                 load_sems, j_send, j_recv, i_send, i_recv, k_send, k_recv, ready):
    J, I, K, L = shape
    chunks = I // rows
    near = {axis: neighbours(sizes, axis) for axis in AXES}
    last_chunks = chunks - jnp.where(is_late(sizes), tail, 0) if tail else chunks

    if any(size % 2 for size in sizes[1:]):
        enter_together(sizes, AXES)
        answer, await_answer = lambda: None, lambda axis: None
    else:
        answer, await_answer = enter(sizes, ready)

    fields = (even, odd)

    def remote(source, target, send, recv, axis, side):
        return pltpu.make_async_remote_copy(
            src_ref=source, dst_ref=target, send_sem=send, recv_sem=recv,
            device_id={axis: near[axis][side]}, device_id_type=MESH)

    def j_copy(step, side, chunk):
        j = (J - 1) * side
        if step == 0:
            source = f_in.at[j, pl.ds(chunk * rows, rows)]
        else:
            source = fields[step % 2].at[j, pl.ds(1 + chunk * rows, rows)]
        return remote(source, jh.at[step, 1 - side, pl.ds(chunk * rows, rows)],
                      j_send.at[step, side, chunk], j_recv.at[step, 1 - side, chunk], "lat", side)

    def i_copy(step, side):
        if step == 0:
            source = f_in.at[:, (I - 1) * side]
        else:
            source = fields[step % 2].at[:, 1 + (I - 1) * side]
        return remote(source, fields[step % 2].at[:, (I + 1) * (1 - side)],
                      i_send.at[step, side], i_recv.at[step, 1 - side], "lon", side)

    def k_copy(step, side):
        return remote(kf.at[step, side], kh.at[step, 1 - side],
                      k_send.at[step, side], k_recv.at[step, 1 - side], "lev", side)

    window = min(WINDOW, chunks - 1 - tail)

    @pl.loop(0, window)
    def _(chunk):
        for side in (0, 1):
            j_copy(0, side, chunk).start()

    answer()
    load_f = pltpu.make_async_copy(f_in, even.at[:, pl.ds(1, I)], load_sems.at[0])
    load_c = pltpu.make_async_copy(c_in, crowd, load_sems.at[1])
    load_f.start()
    load_c.start()
    await_answer("lon")
    for side in (0, 1):
        i_copy(0, side).start()
    load_f.wait()

    @pl.loop(0, I)
    def _(i):
        for j in range(J):
            kf[0, 0, j, pl.ds(i, 1), :] = even[j, i + 1, 0:1, :]
            kf[0, 1, j, pl.ds(i, 1), :] = even[j, i + 1, K - 1:K, :]

    load_c.wait()
    await_answer("lev")
    for side in (0, 1):
        k_copy(0, side).start()

    at_k = lax.broadcasted_iota(jnp.int32, (K, L), 0)

    for step in range(STEPS):
        source, target = fields[step % 2], fields[(step + 1) % 2]
        last = step == STEPS - 1

        def update(i, j, below, above):
            middle = source[j, i + 1]
            total = source[j, i] + source[j, i + 2]
            if below is not None:
                total += below
            if above is not None:
                total += above
            total += jnp.where(at_k == 0, kh[step, 0, j, pl.ds(i, 1), :],
                               pltpu.roll(middle, 1, 0))
            total += jnp.where(at_k == K - 1, kh[step, 1, j, pl.ds(i, 1), :],
                               pltpu.roll(middle, K - 1, 0))
            return middle * (0.6 - 0.2 * (middle * crowd[j, i])) + 0.1 * total

        for side in (0, 1):
            i_copy(step, side).wait_recv()
            k_copy(step, side).wait_recv()
            if step >= 1:
                i_copy(step - 1, side).wait_send()

        if last:
            @pl.loop(window, last_chunks)
            def _(chunk):
                for side in (0, 1):
                    j_copy(step, side, chunk).start()

            @pl.loop(0, I)
            def _(i):
                for j in range(J):
                    target[j, i + 1] = update(
                        i, j, None if j == 0 else source[j - 1, i + 1],
                        None if j == J - 1 else source[j + 1, i + 1])

            @pl.loop(0, last_chunks)
            def _(chunk):
                for side in (0, 1):
                    j_copy(step, side, chunk).wait_recv()
                    j_copy(step, side, chunk).wait_send()

                @pl.loop(0, rows)
                def _(row):
                    i = chunk * rows + row
                    for side in (0, 1):
                        j = (J - 1) * side
                        target[j, i + 1] = target[j, i + 1] + 0.1 * jh[step, side, i]
        else:
            @pl.loop(0, chunks)
            def _(chunk):
                for side in (0, 1):
                    j_copy(step, side, chunk).wait_recv()
                    j_copy(step, side, chunk).wait_send()

                @pl.when(chunk + window < chunks)
                def _():
                    for side in (0, 1):
                        j_copy(step, side, chunk + window).start()

                @pl.when(chunk + window >= chunks)
                def _():
                    for side in (0, 1):
                        j_copy(step + 1, side, chunk + window - chunks).start()

                @pl.loop(0, rows)
                def _(row):
                    i = chunk * rows + row
                    for j in range(J):
                        new = update(
                            i, j, jh[step, 0, i] if j == 0 else source[j - 1, i + 1],
                            jh[step, 1, i] if j == J - 1 else source[j + 1, i + 1])
                        target[j, i + 1] = new
                        kf[step + 1, 0, j, pl.ds(i, 1), :] = new[0:1]
                        kf[step + 1, 1, j, pl.ds(i, 1), :] = new[K - 1:K]

            for side in (0, 1):
                i_copy(step + 1, side).start()
                k_copy(step + 1, side).start()

    for side in (0, 1):
        i_copy(STEPS - 1, side).wait_send()
        for step in range(STEPS):
            k_copy(step, side).wait_send()


def write_kernel(shape, held, out, done, sems):
    J, I = shape[:2]
    copies = [pltpu.make_async_copy(held.at[j, pl.ds(1, I)], out.at[j], sems.at[j])
              for j in range(J)]
    for copy in copies:
        copy.start()
    done[...] = jnp.zeros_like(done)
    for copy in copies:
        copy.wait()


def tail_kernel(sizes, shape, length, rows, done, held, even, fresh, halo, sends, recvs):
    J, I = shape[:2]
    first = I - length
    late = is_late(sizes)

    @pl.when(late)
    def _():
        enter_together(sizes, ("lat",))
        near = neighbours(sizes, "lat")

        def j_copy(side, piece):
            return pltpu.make_async_remote_copy(
                src_ref=even.at[(J - 1) * side, pl.ds(1 + first + piece * rows, rows)],
                dst_ref=halo.at[1 - side, pl.ds(piece * rows, rows)],
                send_sem=sends.at[side, piece], recv_sem=recvs.at[1 - side, piece],
                device_id={"lat": near[side]}, device_id_type=MESH)

        @pl.loop(0, length // rows)
        def _(piece):
            for side in (0, 1):
                j_copy(side, piece).start()

        @pl.loop(0, length // rows)
        def _(piece):
            for side in (0, 1):
                j_copy(side, piece).wait_recv()

            @pl.loop(0, rows)
            def _(row):
                i = piece * rows + row
                for side in (0, 1):
                    fresh[side, i] = held[(J - 1) * side, 1 + first + i] + 0.1 * halo[side, i]

        @pl.loop(0, length // rows)
        def _(piece):
            for side in (0, 1):
                j_copy(side, piece).wait_send()

    @pl.when(jnp.logical_not(late))
    def _():
        @pl.loop(0, length)
        def _(i):
            for side in (0, 1):
                fresh[side, i] = held[(J - 1) * side, 1 + first + i]


def patch_kernel(shape, length, fresh, before, out, sems):
    J, I = shape[:2]
    copies = [pltpu.make_async_copy(fresh.at[side], out.at[(J - 1) * side, pl.ds(I - length, length)],
                                    sems.at[side]) for side in (0, 1)]
    for copy in copies:
        copy.start()
    for copy in copies:
        copy.wait()


def local(sizes, field_values, crowding):
    J, I, K, L = shape = field_values.shape
    rows = math.gcd(I, CHUNK_ROWS)
    chunks = I // rows
    tail = TAIL_CHUNKS if J >= 2 and chunks > TAIL_CHUNKS + 1 else 0
    length = tail * rows
    dtype = field_values.dtype
    DMA = pltpu.SemaphoreType.DMA
    VMEM = pltpu.VMEM
    whole = VMEM((J, I + 2, K, L), dtype)
    in_vmem, anywhere = pl.BlockSpec(memory_space=VMEM), pl.BlockSpec(memory_space=pl.ANY)
    fields = pl.pallas_call(
        functools.partial(march_kernel, sizes, shape, rows, tail),
        out_shape=(whole,) * (2 if tail else 1),
        in_specs=[anywhere] * 2,
        out_specs=(in_vmem,) * (2 if tail else 1),
        scratch_shapes=[whole] * (0 if tail else 1) + [
            VMEM(shape, dtype),
            VMEM((STEPS, 2, I, K, L), dtype),
            VMEM((STEPS, 2, J, I, L), dtype),
            VMEM((STEPS, 2, J, I, L), dtype),
            DMA((2,)),
            DMA((STEPS, 2, chunks)),
            DMA((STEPS, 2, chunks)),
            DMA((STEPS, 2)),
            DMA((STEPS, 2)),
            DMA((STEPS, 2)),
            DMA((STEPS, 2)),
            pltpu.SemaphoreType.REGULAR((len(AXES),)),
        ],
        compiler_params=pltpu.CompilerParams(
            collective_id=0, has_side_effects=True, vmem_limit_bytes=(36 if tail else 50) * 1024 * 1024),
    )(field_values, crowding)
    fields = [pltpu.with_memory_space_constraint(field, VMEM) for field in fields]
    out, done = pl.pallas_call(
        functools.partial(write_kernel, shape),
        out_shape=(jax.ShapeDtypeStruct(shape, dtype), VMEM((8, 128), dtype)),
        in_specs=[in_vmem],
        out_specs=(anywhere, in_vmem),
        scratch_shapes=[DMA((J,))],
        compiler_params=pltpu.CompilerParams(vmem_limit_bytes=1024 * 1024),
    )(fields[0])
    if not tail:
        return out
    piece = math.gcd(length, PIECE_ROWS)
    outer = VMEM((2, length, K, L), dtype)
    fresh = pl.pallas_call(
        functools.partial(tail_kernel, sizes, shape, length, piece),
        out_shape=outer,
        in_specs=[in_vmem] * 3,
        out_specs=in_vmem,
        scratch_shapes=[outer, DMA((2, length // piece)), DMA((2, length // piece))],
        compiler_params=pltpu.CompilerParams(
            collective_id=1, has_side_effects=True, vmem_limit_bytes=4 * 1024 * 1024),
    )(pltpu.with_memory_space_constraint(done, VMEM), *fields)
    return pl.pallas_call(
        functools.partial(patch_kernel, shape, length),
        out_shape=jax.ShapeDtypeStruct(shape, dtype),
        in_specs=[in_vmem, anywhere],
        out_specs=anywhere,
        scratch_shapes=[DMA((2,))],
        input_output_aliases={1: 0},
        compiler_params=pltpu.CompilerParams(vmem_limit_bytes=1024 * 1024),
    )(pltpu.with_memory_space_constraint(fresh, VMEM), out)


def solution(mesh):
    spec = P("lat", "lon", "lev", None)
    sizes = tuple(mesh.shape[axis] for axis in AXES)
    return jax.shard_map(
        functools.partial(local, sizes), mesh=mesh, in_specs=(spec, spec), out_specs=spec,
        check_vma=False,
    )
```

time: 419 us -> 411 us (0.981)
  Pallas kernels: 418 us -> 410 us
    pallas_call x2 -> x4, Pallas kernels: 418 us -> 410 us  [the longest x1 376 us: local(): pl.pallas_call(functools.partial(march_kernel, sizes, shape, rows, tail),...]
where the time goes in v1:
time: 411 us; the launch traced here: 410 us
  Pallas kernels  410 us (100%)
    pallas_call x1, Pallas kernels, local(): pl.pallas_call(functools.partial(march_kernel, sizes, shape, rows, tail),...  376 us
    pallas_call x1, Pallas kernels, local(): pl.pallas_call(functools.partial(tail_kernel, sizes, shape, length, piece...  28.8 us

profile of v1, /device:TPU:1, one launch (start us, length us, event | category | flops | bytes accessed | tf_op | source)
XLA Modules:
  0.0 410.3 jit_solution(13051452300264825416)
XLA Ops:
  0.0 375.6 %shard_map.28 = (f32[4,66,96,128]{3,2,1,0:T(8,128)S(1)}, f32[4,66,96,128]{3,2,1,0:T(8,128)S(1)}) custom-call(f32[4,64,96,128]{3,2,1,0:T(8,128)} %f_in.1, f32[4,64,96,128]{3,2,1,0:T(8,128)} %c_in.1), custom_call_target="tpu_custom_call" | custom-call | tf_op jit(solution)/shard_map/pallas_call | solution.py:295
  375.6 4.7 %shard_map.29 = (f32[4,64,96,128]{3,2,1,0:T(8,128)}, f32[8,128]{1,0:T(8,128)S(1)}) custom-call(f32[4,66,96,128]{3,2,1,0:T(8,128)S(1)} %get-tuple-element.9.held), custom_call_target="tpu_custom_call" | custom-call | tf_op jit(solution)/shard_map/pallas_call | solution.py:318
  380.3 28.8 %shard_map.30.fresh = f32[2,16,96,128]{3,2,1,0:T(8,128)S(1)} custom-call(f32[8,128]{1,0:T(8,128)S(1)} %get-tuple-element.10.done, f32[4,66,96,128]{3,2,1,0:T(8,128)S(1)} %get-tuple-element.9.held, f32[4,66,96,128]{3,2,1,0:T(8,128)S(1)} %get-tuple-element.11.even), custom_call_target="tpu_custom_call" | custom-call | tf_op jit(solution)/shard_map/pallas_call | solution.py:330
  409.1 1.2 shard_map.31

commit v2 on v1

--- a/solution.py
+++ b/solution.py
@@ -33,21 +33,46 @@
 
 def enter(sizes, ready):
     barrier = pltpu.get_barrier_semaphore()
-    second = {axis: lax.rem(lax.axis_index(axis), 2) == parity
-              for axis, parity in (("lon", 1), ("lev", 0))}
-    signal(sizes, "lat", barrier)
-    pl.semaphore_wait(barrier, 2 + sum(2 * second[axis].astype(jnp.int32) for axis in second))
+    odd = lax.rem(lax.axis_index("lat"), 2) == 1
+    follow = lax.rem(lax.axis_index("lev"), 2) == 0
+    before, after = neighbours(sizes, "lat")
+
+    def tell(semaphore, **target):
+        pl.semaphore_signal(semaphore, inc=1, device_id=target, device_id_type=MESH)
+
+    @pl.when(odd)
+    def _():
+        tell(barrier, lat=before)
+
+    @pl.when(jnp.logical_not(odd))
+    def _():
+        tell(barrier, lat=after)
+        tell(barrier, lat=before)
+
+    pl.when(follow)(lambda: signal(sizes, "lon", barrier))
+    pl.semaphore_wait(barrier, 1 + odd.astype(jnp.int32) + 8 * follow.astype(jnp.int32))
+
+    @pl.when(odd)
+    def _():
+        tell(ready.at[0], lat=after)
 
     def answer():
-        for axis in second:
-            pl.when(jnp.logical_not(second[axis]))(lambda: signal(sizes, axis, barrier))
-            pl.when(second[axis])(lambda: signal(sizes, axis, ready.at[AXES.index(axis)]))
-
-    def await_answer(axis):
-        pl.when(jnp.logical_not(second[axis]))(
-            lambda: pl.semaphore_wait(ready.at[AXES.index(axis)], 2))
-
-    return answer, await_answer
+        pl.when(follow)(lambda: signal(sizes, "lev", ready.at[1]))
+
+        @pl.when(jnp.logical_not(follow))
+        def _():
+            signal(sizes, "lev", barrier)
+            for lon in neighbours(sizes, "lon"):
+                for lev in neighbours(sizes, "lev"):
+                    tell(barrier, lon=lon, lev=lev)
+
+    def await_lat():
+        pl.when(jnp.logical_not(odd))(lambda: pl.semaphore_wait(ready.at[0], 1))
+
+    def await_rest():
+        pl.when(jnp.logical_not(follow))(lambda: pl.semaphore_wait(ready.at[1], 2))
+
+    return answer, await_lat, await_rest
 
 
 def enter_together(sizes, axes):
@@ -64,11 +89,11 @@
     near = {axis: neighbours(sizes, axis) for axis in AXES}
     last_chunks = chunks - jnp.where(is_late(sizes), tail, 0) if tail else chunks
 
-    if any(size % 2 for size in sizes[1:]):
+    if sizes[0] % 2 or sizes[2] % 2:
         enter_together(sizes, AXES)
-        answer, await_answer = lambda: None, lambda axis: None
+        answer = await_lat = await_rest = lambda: None
     else:
-        answer, await_answer = enter(sizes, ready)
+        answer, await_lat, await_rest = enter(sizes, ready)
 
     fields = (even, odd)
 
@@ -100,17 +125,21 @@
 
     window = min(WINDOW, chunks - 1 - tail)
 
-    @pl.loop(0, window)
+    j_copy(0, 1, 0).start()
+    answer()
+    await_lat()
+    j_copy(0, 0, 0).start()
+
+    @pl.loop(1, window)
     def _(chunk):
         for side in (0, 1):
             j_copy(0, side, chunk).start()
 
-    answer()
     load_f = pltpu.make_async_copy(f_in, even.at[:, pl.ds(1, I)], load_sems.at[0])
     load_c = pltpu.make_async_copy(c_in, crowd, load_sems.at[1])
     load_f.start()
     load_c.start()
-    await_answer("lon")
+    await_rest()
     for side in (0, 1):
         i_copy(0, side).start()
     load_f.wait()
@@ -122,7 +151,6 @@
             kf[0, 1, j, pl.ds(i, 1), :] = even[j, i + 1, K - 1:K, :]
 
     load_c.wait()
-    await_answer("lev")
     for side in (0, 1):
         k_copy(0, side).start()
 
@@ -228,9 +256,8 @@
 def tail_kernel(sizes, shape, length, rows, done, held, even, fresh, halo, sends, recvs):
     J, I = shape[:2]
     first = I - length
-    late = is_late(sizes)
-
-    @pl.when(late)
+
+    @pl.when(is_late(sizes))
     def _():
         enter_together(sizes, ("lat",))
         near = neighbours(sizes, "lat")
@@ -242,10 +269,13 @@
                 send_sem=sends.at[side, piece], recv_sem=recvs.at[1 - side, piece],
                 device_id={"lat": near[side]}, device_id_type=MESH)
 
+        odd = lax.rem(lax.axis_index("lat"), 2) == 1
+
         @pl.loop(0, length // rows)
         def _(piece):
-            for side in (0, 1):
-                j_copy(side, piece).start()
+            pl.when(odd)(lambda: j_copy(1, piece).start())
+            j_copy(0, piece).start()
+            pl.when(jnp.logical_not(odd))(lambda: j_copy(1, piece).start())
 
         @pl.loop(0, length // rows)
         def _(piece):
@@ -263,22 +293,20 @@
             for side in (0, 1):
                 j_copy(side, piece).wait_send()
 
-    @pl.when(jnp.logical_not(late))
-    def _():
-        @pl.loop(0, length)
-        def _(i):
-            for side in (0, 1):
-                fresh[side, i] = held[(J - 1) * side, 1 + first + i]
-
-
-def patch_kernel(shape, length, fresh, before, out, sems):
+
+def patch_kernel(sizes, shape, length, fresh, before, out, sems):
     J, I = shape[:2]
-    copies = [pltpu.make_async_copy(fresh.at[side], out.at[(J - 1) * side, pl.ds(I - length, length)],
-                                    sems.at[side]) for side in (0, 1)]
-    for copy in copies:
-        copy.start()
-    for copy in copies:
-        copy.wait()
+
+    @pl.when(is_late(sizes))
+    def _():
+        copies = [
+            pltpu.make_async_copy(
+                fresh.at[side], out.at[(J - 1) * side, pl.ds(I - length, length)], sems.at[side])
+            for side in (0, 1)]
+        for copy in copies:
+            copy.start()
+        for copy in copies:
+            copy.wait()
 
 
 def local(sizes, field_values, crowding):
@@ -309,7 +337,7 @@
             DMA((STEPS, 2)),
             DMA((STEPS, 2)),
             DMA((STEPS, 2)),
-            pltpu.SemaphoreType.REGULAR((len(AXES),)),
+            pltpu.SemaphoreType.REGULAR((2,)),
         ],
         compiler_params=pltpu.CompilerParams(
             collective_id=0, has_side_effects=True, vmem_limit_bytes=(36 if tail else 50) * 1024 * 1024),
@@ -337,7 +365,7 @@
             collective_id=1, has_side_effects=True, vmem_limit_bytes=4 * 1024 * 1024),
     )(pltpu.with_memory_space_constraint(done, VMEM), *fields)
     return pl.pallas_call(
-        functools.partial(patch_kernel, shape, length),
+        functools.partial(patch_kernel, sizes, shape, length),
         out_shape=jax.ShapeDtypeStruct(shape, dtype),
         in_specs=[in_vmem, anywhere],
         out_specs=anywhere,

time: 411 us -> 410 us (level)
  no operation moved by 1% of the time
where the time goes in v2:
time: 410 us
  Pallas kernels  410 us (100%)
    pallas_call x1, Pallas kernels, local(): pl.pallas_call(functools.partial(march_kernel, sizes, shape, rows, tail),...  373 us
    pallas_call x1, Pallas kernels, local(): pl.pallas_call(functools.partial(tail_kernel, sizes, shape, length, piece...  31.9 us

profile of v2, /device:TPU:1, one launch (start us, length us, event | category | flops | bytes accessed | tf_op | source)
XLA Modules:
  0.0 410.3 jit_solution(5544416622272104167)
XLA Ops:
  0.0 372.5 %shard_map.28 = (f32[4,66,96,128]{3,2,1,0:T(8,128)S(1)}, f32[4,66,96,128]{3,2,1,0:T(8,128)S(1)}) custom-call(f32[4,64,96,128]{3,2,1,0:T(8,128)} %f_in.1, f32[4,64,96,128]{3,2,1,0:T(8,128)} %c_in.1), custom_call_target="tpu_custom_call" | custom-call | tf_op jit(solution)/shard_map/pallas_call | solution.py:323
  372.5 4.7 %shard_map.29 = (f32[4,64,96,128]{3,2,1,0:T(8,128)}, f32[8,128]{1,0:T(8,128)S(1)}) custom-call(f32[4,66,96,128]{3,2,1,0:T(8,128)S(1)} %get-tuple-element.9.held), custom_call_target="tpu_custom_call" | custom-call | tf_op jit(solution)/shard_map/pallas_call | solution.py:346
  377.2 31.9 %shard_map.30.fresh = f32[2,16,96,128]{3,2,1,0:T(8,128)S(1)} custom-call(f32[8,128]{1,0:T(8,128)S(1)} %get-tuple-element.10.done, f32[4,66,96,128]{3,2,1,0:T(8,128)S(1)} %get-tuple-element.9.held, f32[4,66,96,128]{3,2,1,0:T(8,128)S(1)} %get-tuple-element.11.even), custom_call_target="tpu_custom_call" | custom-call | tf_op jit(solution)/shard_map/pallas_call | solution.py:358
  409.1 1.2 shard_map.31

commit v3 on v2

--- a/solution.py
+++ b/solution.py
@@ -9,9 +9,9 @@
 from jax.sharding import PartitionSpec as P
 
 STEPS = 3
-CHUNK_ROWS = 8
-WINDOW = 5
-TAIL_CHUNKS = 2
+CHUNK_ROWS = 4
+WINDOW = 10
+TAIL_CHUNKS = 3
 PIECE_ROWS = 4
 MESH = pl.DeviceIdType.MESH
 AXES = ("lat", "lon", "lev")
@@ -34,7 +34,11 @@
 def enter(sizes, ready):
     barrier = pltpu.get_barrier_semaphore()
     odd = lax.rem(lax.axis_index("lat"), 2) == 1
-    follow = lax.rem(lax.axis_index("lev"), 2) == 0
+    lead = lax.rem(lax.axis_index("lev"), 2) == 1
+    odd_lon = lax.rem(lax.axis_index("lon"), 2) == 1
+    follow = jnp.logical_not(lead)
+    early = jnp.logical_and(follow, jnp.logical_not(odd_lon))
+    answers = jnp.logical_and(follow, odd_lon)
     before, after = neighbours(sizes, "lat")
 
     def tell(semaphore, **target):
@@ -49,28 +53,32 @@
         tell(barrier, lat=after)
         tell(barrier, lat=before)
 
-    pl.when(follow)(lambda: signal(sizes, "lon", barrier))
-    pl.semaphore_wait(barrier, 1 + odd.astype(jnp.int32) + 8 * follow.astype(jnp.int32))
+    pl.semaphore_wait(barrier, 1 + sum(
+        n * flag.astype(jnp.int32) for n, flag in ((1, odd), (2, follow), (2, answers))))
 
     @pl.when(odd)
     def _():
         tell(ready.at[0], lat=after)
 
     def answer():
-        pl.when(follow)(lambda: signal(sizes, "lev", ready.at[1]))
-
-        @pl.when(jnp.logical_not(follow))
+        pl.when(lead)(lambda: signal(sizes, "lev", barrier))
+        pl.when(early)(lambda: signal(sizes, "lon", barrier))
+
+        @pl.when(answers)
         def _():
-            signal(sizes, "lev", barrier)
-            for lon in neighbours(sizes, "lon"):
-                for lev in neighbours(sizes, "lev"):
-                    tell(barrier, lon=lon, lev=lev)
+            signal(sizes, "lon", ready.at[2])
+            signal(sizes, "lev", ready.at[1])
 
     def await_lat():
         pl.when(jnp.logical_not(odd))(lambda: pl.semaphore_wait(ready.at[0], 1))
 
     def await_rest():
-        pl.when(jnp.logical_not(follow))(lambda: pl.semaphore_wait(ready.at[1], 2))
+        @pl.when(early)
+        def _():
+            pl.semaphore_wait(ready.at[2], 2)
+            signal(sizes, "lev", ready.at[1])
+
+        pl.when(lead)(lambda: pl.semaphore_wait(ready.at[1], 2))
 
     return answer, await_lat, await_rest
 
@@ -89,22 +97,27 @@
     near = {axis: neighbours(sizes, axis) for axis in AXES}
     last_chunks = chunks - jnp.where(is_late(sizes), tail, 0) if tail else chunks
 
-    if sizes[0] % 2 or sizes[2] % 2:
+    fields = (even, odd)
+
+    ahead = pltpu.make_async_copy(
+        f_in.at[J - 1, pl.ds(0, rows)], even.at[J - 1, pl.ds(1, rows)], load_sems.at[2])
+    even_lat = lax.rem(lax.axis_index("lat"), 2) == 0
+    pl.when(even_lat)(ahead.start)
+
+    if any(size % 2 for size in sizes):
         enter_together(sizes, AXES)
         answer = await_lat = await_rest = lambda: None
     else:
         answer, await_lat, await_rest = enter(sizes, ready)
 
-    fields = (even, odd)
-
     def remote(source, target, send, recv, axis, side):
         return pltpu.make_async_remote_copy(
             src_ref=source, dst_ref=target, send_sem=send, recv_sem=recv,
             device_id={axis: near[axis][side]}, device_id_type=MESH)
 
-    def j_copy(step, side, chunk):
+    def j_copy(step, side, chunk, loaded=False):
         j = (J - 1) * side
-        if step == 0:
+        if step == 0 and not loaded:
             source = f_in.at[j, pl.ds(chunk * rows, rows)]
         else:
             source = fields[step % 2].at[j, pl.ds(1 + chunk * rows, rows)]
@@ -125,7 +138,12 @@
 
     window = min(WINDOW, chunks - 1 - tail)
 
-    j_copy(0, 1, 0).start()
+    @pl.when(even_lat)
+    def _():
+        ahead.wait()
+        j_copy(0, 1, 0, loaded=True).start()
+
+    pl.when(jnp.logical_not(even_lat))(lambda: j_copy(0, 1, 0).start())
     answer()
     await_lat()
     j_copy(0, 0, 0).start()
@@ -135,14 +153,22 @@
         for side in (0, 1):
             j_copy(0, side, chunk).start()
 
-    load_f = pltpu.make_async_copy(f_in, even.at[:, pl.ds(1, I)], load_sems.at[0])
+    load_inner = pltpu.make_async_copy(
+        f_in.at[pl.ds(0, J - 1)], even.at[pl.ds(0, J - 1), pl.ds(1, I)], load_sems.at[0])
+    load_outer = pltpu.make_async_copy(
+        f_in.at[J - 1, pl.ds(rows, I - rows)], even.at[J - 1, pl.ds(1 + rows, I - rows)],
+        load_sems.at[3])
     load_c = pltpu.make_async_copy(c_in, crowd, load_sems.at[1])
-    load_f.start()
+    pl.when(jnp.logical_not(even_lat))(ahead.start)
+    load_inner.start()
+    load_outer.start()
     load_c.start()
     await_rest()
     for side in (0, 1):
         i_copy(0, side).start()
-    load_f.wait()
+    pl.when(jnp.logical_not(even_lat))(ahead.wait)
+    load_inner.wait()
+    load_outer.wait()
 
     @pl.loop(0, I)
     def _(i):
@@ -330,14 +356,14 @@
             VMEM((STEPS, 2, I, K, L), dtype),
             VMEM((STEPS, 2, J, I, L), dtype),
             VMEM((STEPS, 2, J, I, L), dtype),
-            DMA((2,)),
+            DMA((4,)),
             DMA((STEPS, 2, chunks)),
             DMA((STEPS, 2, chunks)),
             DMA((STEPS, 2)),
             DMA((STEPS, 2)),
             DMA((STEPS, 2)),
             DMA((STEPS, 2)),
-            pltpu.SemaphoreType.REGULAR((2,)),
+            pltpu.SemaphoreType.REGULAR((3,)),
         ],
         compiler_params=pltpu.CompilerParams(
             collective_id=0, has_side_effects=True, vmem_limit_bytes=(36 if tail else 50) * 1024 * 1024),

time: 410 us -> 410 us (level)
    pallas_call x1, Pallas kernels: 31.9 us -> 19.5 us  [local(): pl.pallas_call(functools.partial(tail_kernel, sizes, shape, length, piece...]
    pallas_call x1, Pallas kernels: 373 us -> 385 us  [local(): pl.pallas_call(functools.partial(march_kernel, sizes, shape, rows, tail),...]
where the time goes in v3:
time: 410 us
  Pallas kernels  410 us (100%)
    pallas_call x1, Pallas kernels, local(): pl.pallas_call(functools.partial(march_kernel, sizes, shape, rows, tail),...  385 us
    pallas_call x1, Pallas kernels, local(): pl.pallas_call(functools.partial(tail_kernel, sizes, shape, length, piece...  19.5 us

profile of v3, /device:TPU:1, one launch (start us, length us, event | category | flops | bytes accessed | tf_op | source)
XLA Modules:
  0.0 410.1 jit_solution(1976808722583858384)
XLA Ops:
  0.0 384.8 %shard_map.28 = (f32[4,66,96,128]{3,2,1,0:T(8,128)S(1)}, f32[4,66,96,128]{3,2,1,0:T(8,128)S(1)}) custom-call(f32[4,64,96,128]{3,2,1,0:T(8,128)} %f_in.1, f32[4,64,96,128]{3,2,1,0:T(8,128)} %c_in.1), custom_call_target="tpu_custom_call" | custom-call | tf_op jit(solution)/shard_map/pallas_call | solution.py:349
  384.8 4.7 %shard_map.29 = (f32[4,64,96,128]{3,2,1,0:T(8,128)}, f32[8,128]{1,0:T(8,128)S(1)}) custom-call(f32[4,66,96,128]{3,2,1,0:T(8,128)S(1)} %get-tuple-element.9.held), custom_call_target="tpu_custom_call" | custom-call | tf_op jit(solution)/shard_map/pallas_call | solution.py:372
  389.6 19.5 %shard_map.30.fresh = f32[2,12,96,128]{3,2,1,0:T(8,128)S(1)} custom-call(f32[8,128]{1,0:T(8,128)S(1)} %get-tuple-element.10.done, f32[4,66,96,128]{3,2,1,0:T(8,128)S(1)} %get-tuple-element.9.held, f32[4,66,96,128]{3,2,1,0:T(8,128)S(1)} %get-tuple-element.11.even), custom_call_target="tpu_custom_call" | custom-call | tf_op jit(solution)/shard_map/pallas_call | solution.py:384
  409.1 1.0 shard_map.31

commit v4 on v3

--- a/solution.py
+++ b/solution.py
@@ -320,15 +320,17 @@
                 j_copy(side, piece).wait_send()
 
 
-def patch_kernel(sizes, shape, length, fresh, before, out, sems):
+def patch_kernel(sizes, shape, length, rows, fresh, before, out, sems):
     J, I = shape[:2]
 
     @pl.when(is_late(sizes))
     def _():
         copies = [
             pltpu.make_async_copy(
-                fresh.at[side], out.at[(J - 1) * side, pl.ds(I - length, length)], sems.at[side])
-            for side in (0, 1)]
+                fresh.at[side, pl.ds(part * rows, rows)],
+                out.at[(J - 1) * side, pl.ds(I - length + part * rows, rows)],
+                sems.at[side, part])
+            for part in range(length // rows) for side in (0, 1)]
         for copy in copies:
             copy.start()
         for copy in copies:
@@ -391,11 +393,11 @@
             collective_id=1, has_side_effects=True, vmem_limit_bytes=4 * 1024 * 1024),
     )(pltpu.with_memory_space_constraint(done, VMEM), *fields)
     return pl.pallas_call(
-        functools.partial(patch_kernel, sizes, shape, length),
+        functools.partial(patch_kernel, sizes, shape, length, piece),
         out_shape=jax.ShapeDtypeStruct(shape, dtype),
         in_specs=[in_vmem, anywhere],
         out_specs=anywhere,
-        scratch_shapes=[DMA((2,))],
+        scratch_shapes=[DMA((2, length // piece))],
         input_output_aliases={1: 0},
         compiler_params=pltpu.CompilerParams(vmem_limit_bytes=1024 * 1024),
     )(pltpu.with_memory_space_constraint(fresh, VMEM), out)

time: 410 us -> 410 us (level)
  no operation moved by 1% of the time
where the time goes in v4:
time: 410 us
  Pallas kernels  410 us (100%)
    pallas_call x1, Pallas kernels, local(): pl.pallas_call(functools.partial(march_kernel, sizes, shape, rows, tail),...  385 us
    pallas_call x1, Pallas kernels, local(): pl.pallas_call(functools.partial(tail_kernel, sizes, shape, length, piece...  19.5 us

profile of v4, /device:TPU:1, one launch (start us, length us, event | category | flops | bytes accessed | tf_op | source)
XLA Modules:
  0.0 410.1 jit_solution(7376184193101967599)
XLA Ops:
  0.0 384.8 %shard_map.28 = (f32[4,66,96,128]{3,2,1,0:T(8,128)S(1)}, f32[4,66,96,128]{3,2,1,0:T(8,128)S(1)}) custom-call(f32[4,64,96,128]{3,2,1,0:T(8,128)} %f_in.1, f32[4,64,96,128]{3,2,1,0:T(8,128)} %c_in.1), custom_call_target="tpu_custom_call" | custom-call | tf_op jit(solution)/shard_map/pallas_call | solution.py:351
  384.8 4.7 %shard_map.29 = (f32[4,64,96,128]{3,2,1,0:T(8,128)}, f32[8,128]{1,0:T(8,128)S(1)}) custom-call(f32[4,66,96,128]{3,2,1,0:T(8,128)S(1)} %get-tuple-element.9.held), custom_call_target="tpu_custom_call" | custom-call | tf_op jit(solution)/shard_map/pallas_call | solution.py:374
  389.6 19.5 %shard_map.30.fresh = f32[2,12,96,128]{3,2,1,0:T(8,128)S(1)} custom-call(f32[8,128]{1,0:T(8,128)S(1)} %get-tuple-element.10.done, f32[4,66,96,128]{3,2,1,0:T(8,128)S(1)} %get-tuple-element.9.held, f32[4,66,96,128]{3,2,1,0:T(8,128)S(1)} %get-tuple-element.11.even), custom_call_target="tpu_custom_call" | custom-call | tf_op jit(solution)/shard_map/pallas_call | solution.py:386
  409.1 1.1 shard_map.31

commit v5 on v4

--- a/solution.py
+++ b/solution.py
@@ -268,15 +268,24 @@
             k_copy(step, side).wait_send()
 
 
-def write_kernel(shape, held, out, done, sems):
+def write_kernel(sizes, shape, length, held, out, done, sems):
     J, I = shape[:2]
-    copies = [pltpu.make_async_copy(held.at[j, pl.ds(1, I)], out.at[j], sems.at[j])
-              for j in range(J)]
-    for copy in copies:
-        copy.start()
+
+    def write(tail):
+        copies = []
+        for j in range(J):
+            count = I - tail if j in (0, J - 1) else I
+            copies.append(pltpu.make_async_copy(
+                held.at[j, pl.ds(1, count)], out.at[j, pl.ds(0, count)], sems.at[j]))
+        for copy in copies:
+            copy.start()
+        for copy in copies:
+            copy.wait()
+
     done[...] = jnp.zeros_like(done)
-    for copy in copies:
-        copy.wait()
+    late = is_late(sizes)
+    pl.when(late)(lambda: write(length))
+    pl.when(jnp.logical_not(late))(lambda: write(0))
 
 
 def tail_kernel(sizes, shape, length, rows, done, held, even, fresh, halo, sends, recvs):
@@ -372,7 +381,7 @@
     )(field_values, crowding)
     fields = [pltpu.with_memory_space_constraint(field, VMEM) for field in fields]
     out, done = pl.pallas_call(
-        functools.partial(write_kernel, shape),
+        functools.partial(write_kernel, sizes, shape, length),
         out_shape=(jax.ShapeDtypeStruct(shape, dtype), VMEM((8, 128), dtype)),
         in_specs=[in_vmem],
         out_specs=(anywhere, in_vmem),

time: 410 us -> 410 us (level)
  no operation moved by 1% of the time
where the time goes in v5:
time: 410 us
  Pallas kernels  410 us (100%)
    pallas_call x1, Pallas kernels, local(): pl.pallas_call(functools.partial(march_kernel, sizes, shape, rows, tail),...  385 us
    pallas_call x1, Pallas kernels, local(): pl.pallas_call(functools.partial(tail_kernel, sizes, shape, length, piece...  19.9 us

profile of v5, /device:TPU:1, one launch (start us, length us, event | category | flops | bytes accessed | tf_op | source)
XLA Modules:
  0.0 410.1 jit_solution(9498126727553887747)
XLA Ops:
  0.0 384.8 %shard_map.28 = (f32[4,66,96,128]{3,2,1,0:T(8,128)S(1)}, f32[4,66,96,128]{3,2,1,0:T(8,128)S(1)}) custom-call(f32[4,64,96,128]{3,2,1,0:T(8,128)} %f_in.1, f32[4,64,96,128]{3,2,1,0:T(8,128)} %c_in.1), custom_call_target="tpu_custom_call" | custom-call | tf_op jit(solution)/shard_map/pallas_call | solution.py:360
  384.8 4.3 %shard_map.29 = (f32[4,64,96,128]{3,2,1,0:T(8,128)}, f32[8,128]{1,0:T(8,128)S(1)}) custom-call(f32[4,66,96,128]{3,2,1,0:T(8,128)S(1)} %get-tuple-element.9.held), custom_call_target="tpu_custom_call" | custom-call | tf_op jit(solution)/shard_map/pallas_call | solution.py:383
  389.2 19.9 %shard_map.30.fresh = f32[2,12,96,128]{3,2,1,0:T(8,128)S(1)} custom-call(f32[8,128]{1,0:T(8,128)S(1)} %get-tuple-element.10.done, f32[4,66,96,128]{3,2,1,0:T(8,128)S(1)} %get-tuple-element.9.held, f32[4,66,96,128]{3,2,1,0:T(8,128)S(1)} %get-tuple-element.11.even), custom_call_target="tpu_custom_call" | custom-call | tf_op jit(solution)/shard_map/pallas_call | solution.py:395
  409.1 1.1 shard_map.31
